TPU v7x, 32 devices: a whole 2x2x4 slice. The times are simulated.
32 devices in a mesh: seq: 32 (over z, y, x, core), head: 1.
Axes of the slice: x: 2, y: 2, z: 4, core: 2. Of those that a mesh axis runs over, the one named last changes fastest.
Arguments:
- queries: bfloat16 [8192, 4096], P('seq', 'head'), may hold values from -8 to 8
- keys: bfloat16 [8192, 1024], P('seq', 'head'), may hold values from -8 to 8
- values: bfloat16 [8192, 1024], P('seq', 'head'), may hold values from -8 to 8
- gate_logit: float32 [32], P('head'), may hold values from -3 to 3
- out_weight: bfloat16 [4096, 4096], P('head'), may hold values from -0.09375 to 0.09375
Outputs:
- layer_out: bfloat16 [8192, 4096], P('seq', 'head')
All inputs are finite; a program needn't handle non-finite values.
Results may differ from a plain program's by a relative error of at most 0.0095.
Values may be sent and summed in bfloat16 or wider, within the bound.
A program may use at most 320 MiB of HBM per device.

v0:
```python
import math

import jax
import jax.numpy as jnp
from jax import lax
from jax.sharding import PartitionSpec as P

HDIM = 128
WINDOW = 4096
SEG = 1024


def from_behind(value, axis, by):
    size = lax.axis_size(axis)
    pairs = [(i, i + by) for i in range(size) if 0 <= i + by < size]
    return lax.ppermute(value, axis, pairs)


def feature(source):
    return jax.nn.elu(source.astype(jnp.float32)) + 1.0


def per_device(queries, keys, values, gate_logit, out_weight):
    row_count = queries.shape[0]
    head_count = gate_logit.shape[0]
    group_count = keys.shape[1] // HDIM
    group_size = head_count // group_count
    score_scale = 1.0 / math.sqrt(HDIM)
    seq_index = lax.axis_index("seq")
    query_four = queries.reshape(row_count, group_count, group_size, HDIM)
    local_row = jnp.arange(row_count, dtype=jnp.int32)
    distance_base = local_row[:, None] - local_row[None, :]

    def attend(state, block_keys, block_values, offset):
        running, sum_total, weighted = state
        key_three = block_keys.reshape(row_count, group_count, HDIM)
        value_three = block_values.reshape(row_count, group_count, HDIM)
        scores = (
            jnp.einsum("tgrd,sgd->tgrs", query_four, key_three, preferred_element_type=jnp.float32)
            * score_scale
        )
        distance = distance_base + offset * row_count
        allowed = (distance >= 0) & (distance < WINDOW) & (seq_index >= offset)
        scores = jnp.where(allowed[:, None, None, :], scores, jnp.float32(-1e30))
        newest = jnp.maximum(running, jnp.max(scores, axis=-1))
        weights = jnp.exp(scores - newest[..., None])
        rescale = jnp.exp(running - newest)
        sum_total = sum_total * rescale + jnp.sum(weights, axis=-1)
        product = jnp.einsum(
            "tgrs,sgd->tgrd",
            weights.astype(jnp.bfloat16),
            value_three,
            preferred_element_type=jnp.float32,
        )
        weighted = weighted * rescale[..., None] + product
        return (newest, sum_total, weighted)

    state = (
        jnp.full((row_count, group_count, group_size), -1e30, jnp.float32),
        jnp.zeros((row_count, group_count, group_size), jnp.float32),
        jnp.zeros((row_count, group_count, group_size, HDIM), jnp.float32),
    )
    state = attend(state, keys, values, 0)
    moving = (keys, values)
    for offset in range(1, WINDOW // row_count + 1):
        moving = from_behind((moving[0], moving[1]), "seq", 1)
        state = attend(state, moving[0], moving[1], offset)
    local_out = state[2] / state[1][..., None]
    key_feature = feature(keys).astype(jnp.bfloat16).reshape(row_count, group_count, HDIM)
    value_three = values.reshape(row_count, group_count, HDIM)
    delta_memory = jnp.einsum(
        "sgd,sge->gde", key_feature, value_three, preferred_element_type=jnp.float32
    )
    delta_norm = jnp.sum(key_feature.astype(jnp.float32), axis=0)
    per_segment = SEG // row_count
    zero_memory = jnp.zeros_like(delta_memory)
    zero_norm = jnp.zeros_like(delta_norm)
    seg_start = seq_index - seq_index % per_segment
    pieces = (
        lax.all_gather(delta_memory[None].astype(jnp.bfloat16), "seq", axis=0, tiled=True).astype(
            jnp.float32
        ),
        lax.all_gather(delta_norm[None].astype(jnp.bfloat16), "seq", axis=0, tiled=True).astype(
            jnp.float32
        ),
    )
    piece_rows = pieces[0].shape[0]
    keep_mask = (jnp.arange(piece_rows, dtype=jnp.int32) < seg_start).astype(jnp.float32)
    memory_part = jnp.einsum("n,ngde->gde", keep_mask, pieces[0], precision=lax.Precision.HIGHEST)
    norm_part = jnp.einsum("n,ngd->gd", keep_mask, pieces[1], precision=lax.Precision.HIGHEST)
    memory = zero_memory + memory_part
    key_total = zero_norm + norm_part
    query_feature = (
        feature(queries)
        .astype(jnp.bfloat16)
        .astype(jnp.float32)
        .reshape(row_count, group_count, group_size, HDIM)
    )
    recalled = jnp.einsum("tgrd,gde->tgre", query_feature, memory, precision=lax.Precision.HIGHEST)
    denominator = 1.0 + jnp.einsum(
        "tgrd,gd->tgr", query_feature, key_total, precision=lax.Precision.HIGHEST
    )
    retrieved = recalled / denominator[..., None]
    gate_share = jax.nn.sigmoid(gate_logit).reshape(group_count, group_size)[None, :, :, None]
    mixed = (gate_share * retrieved + (1.0 - gate_share) * local_out).astype(jnp.bfloat16)
    mixed = mixed.reshape(row_count, head_count * HDIM)
    partial_value = jnp.dot(mixed, out_weight, preferred_element_type=jnp.float32)
    return lax.psum_scatter(
        partial_value.astype(jnp.bfloat16), "head", scatter_dimension=1, tiled=True
    )


def solution(mesh):
    in_specs = (P("seq", "head"), P("seq", "head"), P("seq", "head"), P("head"), P("head", None))
    out_specs = P("seq", "head")
    return jax.shard_map(
        per_device, mesh=mesh, in_specs=in_specs, out_specs=out_specs, check_vma=False
    )
```

profile of v0, /device:TPU:0, one launch (start us, length us, event | category | flops | bytes accessed | tf_op | source)
XLA Modules:
  0.0 575.1 jit_solution(3061893449885910473)
XLA Ops:
  46.0 10.9 %collective-permute-start.7 = (bf16[256,1024]{1,0:T(8,128)(2,1)}, bf16[256,1024]{1,0:T(8,128)(2,1)}, u32[]{:S(2)}, u32[]{:S(2)}) collective-permute-start(bf16[256,1024]{1,0:T(8,128)(2,1)} %collective-permute-done.5), channel_id=1, source_target_pairs={{0,1},{1,2},{2,3},{3,4},{4,5},{5,6},{6,7},{7,8},{8,9},{9,10},{10,1... | collective-permute-start | bytes 1572872 | tf_op jit(solution)/shard_map/ppermute | solution.py:16
  60.3 66.8 %all_gather.7 = bf16[32,8,128]{2,1,0:T(8,128)(2,1)S(1)} all-gather(bf16[1,8,128]{2,1,0:T(8,128)(2,1)S(1)} %bitcast.603), channel_id=1, replica_groups=mesh['seq'=32,'head'=1] {'seq'}, dimensions={0}, use_global_device_ids=true | all-gather | bytes 67584 | tf_op jit(solution)/shard_map/all_gather | solution.py:83
  171.6 7.0 %fusion.36 = (f32[256,8,4]{0,2,1:T(4,128)}, f32[8,256,256,4]{2,1,3,0:T(8,128)}) fusion(pred[256,256]{0,1:T(8,128)(4,1)} %fusion.272, bf16[256,8,4,128]{3,2,1,0:T(4,128)(2,1)S(1)} %reshape.1131, bf16[256,8,128,1]{2,1,0,3:T(8,128)(2,1)S(1)} %bitcast.597), kind=kOutput, calls=%fused_computation.72 | convolution fusion | flops 543154176 | bytes 11108352 | tf_op jit(solution)/shard_map/tgrd,sgd->tgrs/dot_general | solution.py:39
  235.1 7.1 %fusion.41 = (f32[256,8,4]{0,2,1:T(4,128)}, f32[8,256,256,4]{2,1,3,0:T(8,128)}) fusion(pred[256,256]{0,1:T(8,128)(4,1)S(1)} %copy-done.31, bf16[256,8,128,1]{0,2,3,1:T(8,128)(2,1)} %bitcast.600, bf16[256,8,4,128]{3,2,1,0:T(4,128)(2,1)S(1)} %reshape.1131), kind=kOutput, calls=%fused_computation.77 | convolution fusion | flops 543154176 | bytes 11108352 | tf_op jit(solution)/shard_map/tgrd,sgd->tgrs/dot_general | solution.py:39
  246.4 7.1 %fusion.42 = (f32[256,8,4]{0,2,1:T(4,128)}, f32[8,256,256,4]{2,1,3,0:T(8,128)}) fusion(pred[256,256]{0,1:T(8,128)(4,1)S(1)} %copy-done.29, bf16[256,8,128,1]{0,2,3,1:T(8,128)(2,1)} %bitcast.154, bf16[256,8,4,128]{3,2,1,0:T(4,128)(2,1)S(1)} %reshape.1131), kind=kOutput, calls=%fused_computation.78 | convolution fusion | flops 543154176 | bytes 11108352 | tf_op jit(solution)/shard_map/tgrd,sgd->tgrs/dot_general | solution.py:39
  257.7 7.2 %fusion.43 = (f32[256,8,4]{0,2,1:T(4,128)}, f32[8,256,256,4]{2,1,3,0:T(8,128)}) fusion(pred[256,256]{0,1:T(8,128)(4,1)S(1)} %copy-done.23, bf16[256,8,128,1]{0,2,3,1:T(8,128)(2,1)} %bitcast.158, bf16[256,8,4,128]{3,2,1,0:T(4,128)(2,1)S(1)} %reshape.1131), kind=kOutput, calls=%fused_computation.79 | convolution fusion | flops 543154176 | bytes 11108352 | tf_op jit(solution)/shard_map/tgrd,sgd->tgrs/dot_general | solution.py:39
  269.1 7.2 %fusion.44 = (f32[256,8,4]{0,2,1:T(4,128)}, f32[8,256,256,4]{2,1,3,0:T(8,128)}) fusion(pred[256,256]{0,1:T(8,128)(4,1)S(1)} %copy-done.19, bf16[256,8,128,1]{0,2,3,1:T(8,128)(2,1)} %bitcast.162, bf16[256,8,4,128]{3,2,1,0:T(4,128)(2,1)S(1)} %reshape.1131), kind=kOutput, calls=%fused_computation.80 | convolution fusion | flops 543154176 | bytes 11108352 | tf_op jit(solution)/shard_map/tgrd,sgd->tgrs/dot_general | solution.py:39
  280.7 7.2 %fusion.45 = (f32[256,8,4]{0,2,1:T(4,128)}, f32[8,256,256,4]{2,1,3,0:T(8,128)}) fusion(pred[256,256]{0,1:T(8,128)(4,1)S(1)} %copy-done.21, bf16[256,8,128,1]{0,2,3,1:T(8,128)(2,1)} %bitcast.166, bf16[256,8,4,128]{3,2,1,0:T(4,128)(2,1)S(1)} %reshape.1131), kind=kOutput, calls=%fused_computation.81 | convolution fusion | flops 543154176 | bytes 11108352 | tf_op jit(solution)/shard_map/tgrd,sgd->tgrs/dot_general | solution.py:39
  292.9 7.1 %fusion.46 = (f32[256,8,4]{0,2,1:T(4,128)}, f32[8,256,256,4]{2,1,3,0:T(8,128)}) fusion(pred[256,256]{0,1:T(8,128)(4,1)S(1)} %copy-done.25, bf16[256,8,128,1]{0,2,3,1:T(8,128)(2,1)} %bitcast.170, bf16[256,8,4,128]{3,2,1,0:T(4,128)(2,1)S(1)} %reshape.1131), kind=kOutput, calls=%fused_computation.82 | convolution fusion | flops 543154176 | bytes 11108352 | tf_op jit(solution)/shard_map/tgrd,sgd->tgrs/dot_general | solution.py:39
  305.7 7.0 %fusion.47 = (f32[256,8,4]{0,2,1:T(4,128)}, f32[8,256,256,4]{2,1,3,0:T(8,128)}) fusion(pred[256,256]{0,1:T(8,128)(4,1)S(1)} %fusion.250, bf16[256,8,128,1]{0,2,3,1:T(8,128)(2,1)} %bitcast.174, bf16[256,8,4,128]{3,2,1,0:T(4,128)(2,1)S(1)} %reshape.1131), kind=kOutput, calls=%fused_computation.83 | convolution fusion | flops 543154176 | bytes 11108352 | tf_op jit(solution)/shard_map/tgrd,sgd->tgrs/dot_general | solution.py:39
  319.8 7.1 %fusion.48 = (f32[256,8,4]{0,2,1:T(4,128)}, f32[8,256,256,4]{2,1,3,0:T(8,128)}) fusion(pred[256,256]{0,1:T(8,128)(4,1)S(1)} %fusion.248, bf16[256,8,128,1]{0,2,3,1:T(8,128)(2,1)} %bitcast.178, bf16[256,8,4,128]{3,2,1,0:T(4,128)(2,1)S(1)} %reshape.1131), kind=kOutput, calls=%fused_computation.84 | convolution fusion | flops 543154176 | bytes 11108352 | tf_op jit(solution)/shard_map/tgrd,sgd->tgrs/dot_general | solution.py:39
  332.8 7.1 %fusion.49 = (f32[256,8,4]{0,2,1:T(4,128)}, f32[8,256,256,4]{2,1,3,0:T(8,128)}) fusion(pred[256,256]{0,1:T(8,128)(4,1)S(1)} %fusion.246, bf16[256,8,128,1]{0,2,3,1:T(8,128)(2,1)} %bitcast.182, bf16[256,8,4,128]{3,2,1,0:T(4,128)(2,1)S(1)} %reshape.1131), kind=kOutput, calls=%fused_computation.85 | convolution fusion | flops 543154176 | bytes 11108352 | tf_op jit(solution)/shard_map/tgrd,sgd->tgrs/dot_general | solution.py:39
  344.0 7.1 %fusion.50 = (f32[256,8,4]{0,2,1:T(4,128)}, f32[8,256,256,4]{2,1,3,0:T(8,128)}) fusion(pred[256,256]{0,1:T(8,128)(4,1)S(1)} %fusion.244, bf16[256,8,128,1]{0,2,3,1:T(8,128)(2,1)} %bitcast.186, bf16[256,8,4,128]{3,2,1,0:T(4,128)(2,1)S(1)} %reshape.1131), kind=kOutput, calls=%fused_computation.86 | convolution fusion | flops 543154176 | bytes 11108352 | tf_op jit(solution)/shard_map/tgrd,sgd->tgrs/dot_general | solution.py:39
  369.8 9.0 %fusion.2 = (f32[256,8,4]{0,2,1:T(4,128)}, f32[256,8,4]{0,2,1:T(4,128)}) fusion(f32[8,256,256,4]{2,1,3,0:T(8,128)S(1)} %bitcast.537, f32[256,8,4]{0,2,1:T(4,128)S(1)} %get-tuple-element.41, pred[256,256]{0,1:T(8,128)(4,1)S(1)} %copy-done.27, f32[256,8,4]{0,2,1:T(4,128)S(1)} %get-tuple-element.39, f32[8,256,256,4]{2,1,3,0:T(8,128)} %get-tuple-element.73, ...), kind=kLoop, calls=%fused_computation.38 | loop fusion | flops 16760832 | bytes 17039360 | tf_op jit(solution)/shard_map/reduce_sum | solution.py:48
  378.9 7.3 %fusion.6 = (f32[256,8,4]{0,2,1:T(4,128)}, f32[256,8,4]{0,2,1:T(4,128)}) fusion(f32[8,256,256,4]{2,1,3,0:T(8,128)S(1)} %bitcast.543, f32[256,8,4]{0,2,1:T(4,128)S(1)} %get-tuple-element.38, pred[256,256]{0,1:T(8,128)(4,1)S(1)} %copy-done.37, f32[256,8,4]{0,2,1:T(4,128)S(1)} %get-tuple-element.37, f32[8,256,256,4]{2,1,3,0:T(8,128)} %get-tuple-element.69, ...), kind=kLoop, calls=%fused_computation.42 | loop fusion | flops 16760832 | bytes 17039360 | tf_op jit(solution)/shard_map/reduce_sum | solution.py:48
  386.3 7.2 %fusion.10 = (f32[256,8,4]{0,2,1:T(4,128)}, f32[256,8,4]{0,2,1:T(4,128)}) fusion(f32[8,256,256,4]{2,1,3,0:T(8,128)S(1)} %bitcast.549, f32[256,8,4]{0,2,1:T(4,128)S(1)} %get-tuple-element.36, pred[256,256]{0,1:T(8,128)(4,1)S(1)} %copy-done.34, f32[256,8,4]{0,2,1:T(4,128)S(1)} %get-tuple-element.35, f32[8,256,256,4]{2,1,3,0:T(8,128)} %get-tuple-element.65, ...), kind=kLoop, calls=%fused_computation.46 | loop fusion | flops 16760832 | bytes 17039360 | tf_op jit(solution)/shard_map/reduce_sum | solution.py:48
  396.7 8.2 %fusion.14 = (f32[256,8,4]{0,2,1:T(4,128)S(1)}, f32[256,8,4]{0,2,1:T(4,128)S(1)}) fusion(f32[8,256,256,4]{2,1,3,0:T(8,128)} %get-tuple-element.63, f32[256,8,4]{0,2,1:T(4,128)S(1)} %copy-done.58, pred[256,256]{0,1:T(8,128)(4,1)S(1)} %copy-done.30, f32[256,8,4]{0,2,1:T(4,128)S(1)} %copy-done.60, f32[8,256,256,4]{2,1,3,0:T(8,128)} %get-tuple-element.61, ...), kind=kLoop, calls=%fused_computation.50 | loop fusion | flops 16760832 | bytes 17039360 | tf_op jit(solution)/shard_map/reduce_sum | solution.py:48
  405.1 8.3 %fusion.18 = (f32[256,8,4]{0,2,1:T(4,128)S(1)}, f32[256,8,4]{0,2,1:T(4,128)S(1)}) fusion(f32[8,256,256,4]{2,1,3,0:T(8,128)} %get-tuple-element.59, f32[256,8,4]{0,2,1:T(4,128)S(1)} %copy-done.61, pred[256,256]{0,1:T(8,128)(4,1)S(1)} %copy-done.20, f32[256,8,4]{0,2,1:T(4,128)S(1)} %copy-done.62, f32[8,256,256,4]{2,1,3,0:T(8,128)} %get-tuple-element.57, ...), kind=kLoop, calls=%fused_computation.54 | loop fusion | flops 16760832 | bytes 17039360 | tf_op jit(solution)/shard_map/reduce_sum | solution.py:48
  432.4 7.7 %fusion.65 = f32[8,256,4,128]{1,3,2,0:T(8,128)} fusion(bf16[256,8,128,1]{0,2,3,1:T(8,128)(2,1)S(1)} %bitcast.593, f32[8,256,256,4]{2,1,3,0:T(8,128)} %get-tuple-element.55, f32[256,8,4]{0,2,1:T(4,128)S(1)} %copy-done.63, pred[256,256]{0,1:T(8,128)(4,1)S(1)} %copy-done.26), kind=kOutput, calls=%fused_computation.96 | convolution fusion | flops 545259520 | bytes 13205504 | tf_op jit(solution)/shard_map/tgrs,sgd->tgrd/dot_general | solution.py:49
  440.2 7.7 %fusion.67 = f32[8,256,4,128]{1,3,2,0:T(8,128)} fusion(bf16[256,8,128,1]{0,2,3,1:T(8,128)(2,1)S(1)} %bitcast.589, f32[8,256,256,4]{2,1,3,0:T(8,128)} %get-tuple-element.57, f32[256,8,4]{0,2,1:T(4,128)S(1)} %copy-done.62, pred[256,256]{0,1:T(8,128)(4,1)S(1)} %copy-done.22), kind=kOutput, calls=%fused_computation.97 | convolution fusion | flops 545259520 | bytes 13205504 | tf_op jit(solution)/shard_map/tgrs,sgd->tgrd/dot_general | solution.py:49
  456.4 7.7 %fusion.63 = f32[8,256,4,128]{1,3,2,0:T(8,128)} fusion(bf16[256,8,128,1]{0,2,3,1:T(8,128)(2,1)S(1)} %bitcast.592, f32[8,256,256,4]{2,1,3,0:T(8,128)} %get-tuple-element.53, f32[256,8,4]{0,2,1:T(4,128)S(1)} %copy-done.59, pred[256,256]{0,1:T(8,128)(4,1)S(1)} %fusion.250), kind=kOutput, calls=%fused_computation.95 | convolution fusion | flops 545259520 | bytes 13205504 | tf_op jit(solution)/shard_map/tgrs,sgd->tgrd/dot_general | solution.py:49
  511.1 8.3 %fusion = f32[1,8,128,128]{3,0,2,1:T(1,128)S(1)} fusion(bf16[32,8,128,128]{3,2,1,0:T(8,128)(2,1)} %bitcast.575, s32[]{:T(128)S(6)} %sub.481), kind=kOutput, calls=%fused_computation.19 | convolution fusion | flops 8388640 | bytes 8912900 | tf_op jit(solution)/shard_map/n,ngde->gde/dot_general | solution.py:89
  525.8 25.3 %fusion.178 = bf16[256,8,4,128]{0,3,2,1:T(8,128)(2,1)} fusion(f32[8,256,4,128]{1,3,2,0:T(8,128)} %fusion.55, f32[8,256,4,128]{1,3,2,0:T(8,128)} %fusion.57, f32[8,256,4,128]{1,3,2,0:T(8,128)} %fusion.59, f32[8,256,4,128]{1,3,2,0:T(8,128)} %fusion.61, f32[8,256,4,128]{1,3,2,0:T(8,128)} %fusion.63, f32[8,256,4,128]{1,3,2,0:T(8,128)} %fusion.65, ...), kind=kOutput, calls=%fused_computation.217 | convolution fusion | flops 586153984 | bytes 83034368 | tf_op jit(solution)/shard_map/tgrs,sgd->tgrd/dot_general | solution.py:49
  551.2 16.6 %convolution_convert_fusion = bf16[256,4096]{1,0:T(8,128)(2,1)} fusion(bf16[256,4096]{0,1:T(8,128)(2,1)} %bitcast.574, bf16[4096,4096]{1,0:T(8,128)(2,1)} %param.9), kind=kOutput, calls=%fused_computation.89 | convolution fusion | flops 8590983168 | bytes 37748736 | tf_op jit(solution)/shard_map/dot_general | solution.py:107
  (465 shorter events, 290.0 us)
Async XLA Ops:
  6.5 504.5 %all-gather.3.cloned.1.call-start = ((), (), s32[]{:S(2)}) async-start(), calls=%async_computation | async-start | bytes 8650752 | tf_op jit(solution)/shard_map/all_gather | solution.py:80
  20.9 15.7 %collective-permute-start.3 = (bf16[256,1024]{1,0:T(8,128)(2,1)S(1)}, bf16[256,1024]{1,0:T(8,128)(2,1)S(1)}, u32[]{:S(2)}, u32[]{:S(2)}) collective-permute-start(bf16[256,1024]{1,0:T(8,128)(2,1)S(1)} %collective-permute-done.1), channel_id=1, source_target_pairs={{0,1},{1,2},{2,3},{3,4},{4,5},{5,6},{6,7},{7,8},{8,9},{9,10},{10,1... | collective-permute-start | bytes 1572872 | tf_op jit(solution)/shard_map/ppermute | solution.py:16
  40.4 88.6 %collective-permute-start.6 = (bf16[256,1024]{0,1:T(8,128)(2,1)}, bf16[256,1024]{0,1:T(8,128)(2,1)}, u32[]{:S(2)}, u32[]{:S(2)}) collective-permute-start(bf16[256,1024]{0,1:T(8,128)(2,1)} %collective-permute-done.4), channel_id=1, source_target_pairs={{0,1},{1,2},{2,3},{3,4},{4,5},{5,6},{6,7},{7,8},{8,9},{9,10},{10,1... | collective-permute-start | bytes 1572872 | tf_op jit(solution)/shard_map/ppermute | solution.py:16
  46.0 85.9 %collective-permute-start.7 = (bf16[256,1024]{1,0:T(8,128)(2,1)}, bf16[256,1024]{1,0:T(8,128)(2,1)}, u32[]{:S(2)}, u32[]{:S(2)}) collective-permute-start(bf16[256,1024]{1,0:T(8,128)(2,1)} %collective-permute-done.5), channel_id=1, source_target_pairs={{0,1},{1,2},{2,3},{3,4},{4,5},{5,6},{6,7},{7,8},{8,9},{9,10},{10,1... | collective-permute-start | bytes 1572872 | tf_op jit(solution)/shard_map/ppermute | solution.py:16
  136.2 13.9 %collective-permute-start.10 = (bf16[256,1024]{0,1:T(8,128)(2,1)S(1)}, bf16[256,1024]{0,1:T(8,128)(2,1)}, u32[]{:S(2)}, u32[]{:S(2)}) collective-permute-start(bf16[256,1024]{0,1:T(8,128)(2,1)S(1)} %collective-permute-done.8), channel_id=1, source_target_pairs={{0,1},{1,2},{2,3},{3,4},{4,5},{5,6},{6,7},{7,8},{8,9},{9,10},{10,1... | collective-permute-start | bytes 1572872 | tf_op jit(solution)/shard_map/ppermute | solution.py:16
  154.9 14.4 %collective-permute-start.13 = (bf16[256,1024]{1,0:T(8,128)(2,1)}, bf16[256,1024]{1,0:T(8,128)(2,1)}, u32[]{:S(2)}, u32[]{:S(2)}) collective-permute-start(bf16[256,1024]{1,0:T(8,128)(2,1)} %collective-permute-done.11), channel_id=1, source_target_pairs={{0,1},{1,2},{2,3},{3,4},{4,5},{5,6},{6,7},{7,8},{8,9},{9,10},{10,1... | collective-permute-start | bytes 1572872 | tf_op jit(solution)/shard_map/ppermute | solution.py:16
  160.9 17.7 %collective-permute-start.14 = (bf16[256,1024]{0,1:T(8,128)(2,1)}, bf16[256,1024]{0,1:T(8,128)(2,1)}, u32[]{:S(2)}, u32[]{:S(2)}) collective-permute-start(bf16[256,1024]{0,1:T(8,128)(2,1)} %collective-permute-done.12), channel_id=1, source_target_pairs={{0,1},{1,2},{2,3},{3,4},{4,5},{5,6},{6,7},{7,8},{8,9},{9,10},{10,1... | collective-permute-start | bytes 1572872 | tf_op jit(solution)/shard_map/ppermute | solution.py:16
  169.3 15.5 %collective-permute-start.15 = (bf16[256,1024]{1,0:T(8,128)(2,1)}, bf16[256,1024]{1,0:T(8,128)(2,1)}, u32[]{:S(2)}, u32[]{:S(2)}) collective-permute-start(bf16[256,1024]{1,0:T(8,128)(2,1)} %collective-permute-done.13), channel_id=1, source_target_pairs={{0,1},{1,2},{2,3},{3,4},{4,5},{5,6},{6,7},{7,8},{8,9},{9,10},{10,1... | collective-permute-start | bytes 1572872 | tf_op jit(solution)/shard_map/ppermute | solution.py:16
  178.6 17.2 %collective-permute-start.16 = (bf16[256,1024]{0,1:T(8,128)(2,1)}, bf16[256,1024]{0,1:T(8,128)(2,1)}, u32[]{:S(2)}, u32[]{:S(2)}) collective-permute-start(bf16[256,1024]{0,1:T(8,128)(2,1)} %collective-permute-done.14), channel_id=1, source_target_pairs={{0,1},{1,2},{2,3},{3,4},{4,5},{5,6},{6,7},{7,8},{8,9},{9,10},{10,1... | collective-permute-start | bytes 1572872 | tf_op jit(solution)/shard_map/ppermute | solution.py:16
  184.8 21.6 %collective-permute-start.17 = (bf16[256,1024]{1,0:T(8,128)(2,1)}, bf16[256,1024]{1,0:T(8,128)(2,1)}, u32[]{:S(2)}, u32[]{:S(2)}) collective-permute-start(bf16[256,1024]{1,0:T(8,128)(2,1)} %collective-permute-done.15), channel_id=1, source_target_pairs={{0,1},{1,2},{2,3},{3,4},{4,5},{5,6},{6,7},{7,8},{8,9},{9,10},{10,1... | collective-permute-start | bytes 1572872 | tf_op jit(solution)/shard_map/ppermute | solution.py:16
  195.8 22.2 %collective-permute-start.18 = (bf16[256,1024]{0,1:T(8,128)(2,1)}, bf16[256,1024]{0,1:T(8,128)(2,1)}, u32[]{:S(2)}, u32[]{:S(2)}) collective-permute-start(bf16[256,1024]{0,1:T(8,128)(2,1)} %collective-permute-done.16), channel_id=1, source_target_pairs={{0,1},{1,2},{2,3},{3,4},{4,5},{5,6},{6,7},{7,8},{8,9},{9,10},{10,1... | collective-permute-start | bytes 1572872 | tf_op jit(solution)/shard_map/ppermute | solution.py:16
  206.4 25.1 %collective-permute-start.19 = (bf16[256,1024]{1,0:T(8,128)(2,1)}, bf16[256,1024]{1,0:T(8,128)(2,1)}, u32[]{:S(2)}, u32[]{:S(2)}) collective-permute-start(bf16[256,1024]{1,0:T(8,128)(2,1)} %collective-permute-done.17), channel_id=1, source_target_pairs={{0,1},{1,2},{2,3},{3,4},{4,5},{5,6},{6,7},{7,8},{8,9},{9,10},{10,1... | collective-permute-start | bytes 1572872 | tf_op jit(solution)/shard_map/ppermute | solution.py:16
  218.0 26.3 %collective-permute-start.20 = (bf16[256,1024]{0,1:T(8,128)(2,1)}, bf16[256,1024]{0,1:T(8,128)(2,1)}, u32[]{:S(2)}, u32[]{:S(2)}) collective-permute-start(bf16[256,1024]{0,1:T(8,128)(2,1)} %collective-permute-done.18), channel_id=1, source_target_pairs={{0,1},{1,2},{2,3},{3,4},{4,5},{5,6},{6,7},{7,8},{8,9},{9,10},{10,1... | collective-permute-start | bytes 1572872 | tf_op jit(solution)/shard_map/ppermute | solution.py:16
  231.5 24.1 %collective-permute-start.21 = (bf16[256,1024]{1,0:T(8,128)(2,1)}, bf16[256,1024]{1,0:T(8,128)(2,1)}, u32[]{:S(2)}, u32[]{:S(2)}) collective-permute-start(bf16[256,1024]{1,0:T(8,128)(2,1)} %collective-permute-done.19), channel_id=1, source_target_pairs={{0,1},{1,2},{2,3},{3,4},{4,5},{5,6},{6,7},{7,8},{8,9},{9,10},{10,1... | collective-permute-start | bytes 1572872 | tf_op jit(solution)/shard_map/ppermute | solution.py:16
  244.3 22.7 %collective-permute-start.22 = (bf16[256,1024]{0,1:T(8,128)(2,1)}, bf16[256,1024]{0,1:T(8,128)(2,1)}, u32[]{:S(2)}, u32[]{:S(2)}) collective-permute-start(bf16[256,1024]{0,1:T(8,128)(2,1)} %collective-permute-done.20), channel_id=1, source_target_pairs={{0,1},{1,2},{2,3},{3,4},{4,5},{5,6},{6,7},{7,8},{8,9},{9,10},{10,1... | collective-permute-start | bytes 1572872 | tf_op jit(solution)/shard_map/ppermute | solution.py:16
  255.6 22.8 %collective-permute-start.23 = (bf16[256,1024]{1,0:T(8,128)(2,1)}, bf16[256,1024]{1,0:T(8,128)(2,1)}, u32[]{:S(2)}, u32[]{:S(2)}) collective-permute-start(bf16[256,1024]{1,0:T(8,128)(2,1)} %collective-permute-done.21), channel_id=1, source_target_pairs={{0,1},{1,2},{2,3},{3,4},{4,5},{5,6},{6,7},{7,8},{8,9},{9,10},{10,1... | collective-permute-start | bytes 1572872 | tf_op jit(solution)/shard_map/ppermute | solution.py:16
  267.0 22.9 %collective-permute-start.24 = (bf16[256,1024]{0,1:T(8,128)(2,1)}, bf16[256,1024]{0,1:T(8,128)(2,1)}, u32[]{:S(2)}, u32[]{:S(2)}) collective-permute-start(bf16[256,1024]{0,1:T(8,128)(2,1)} %collective-permute-done.22), channel_id=1, source_target_pairs={{0,1},{1,2},{2,3},{3,4},{4,5},{5,6},{6,7},{7,8},{8,9},{9,10},{10,1... | collective-permute-start | bytes 1572872 | tf_op jit(solution)/shard_map/ppermute | solution.py:16
  278.4 23.7 %collective-permute-start.25 = (bf16[256,1024]{1,0:T(8,128)(2,1)}, bf16[256,1024]{1,0:T(8,128)(2,1)}, u32[]{:S(2)}, u32[]{:S(2)}) collective-permute-start(bf16[256,1024]{1,0:T(8,128)(2,1)} %collective-permute-done.23), channel_id=1, source_target_pairs={{0,1},{1,2},{2,3},{3,4},{4,5},{5,6},{6,7},{7,8},{8,9},{9,10},{10,1... | collective-permute-start | bytes 1572872 | tf_op jit(solution)/shard_map/ppermute | solution.py:16
  289.9 24.9 %collective-permute-start.26 = (bf16[256,1024]{0,1:T(8,128)(2,1)}, bf16[256,1024]{0,1:T(8,128)(2,1)}, u32[]{:S(2)}, u32[]{:S(2)}) collective-permute-start(bf16[256,1024]{0,1:T(8,128)(2,1)} %collective-permute-done.24), channel_id=1, source_target_pairs={{0,1},{1,2},{2,3},{3,4},{4,5},{5,6},{6,7},{7,8},{8,9},{9,10},{10,1... | collective-permute-start | bytes 1572872 | tf_op jit(solution)/shard_map/ppermute | solution.py:16
  302.1 26.9 %collective-permute-start.27 = (bf16[256,1024]{1,0:T(8,128)(2,1)}, bf16[256,1024]{1,0:T(8,128)(2,1)}, u32[]{:S(2)}, u32[]{:S(2)}) collective-permute-start(bf16[256,1024]{1,0:T(8,128)(2,1)} %collective-permute-done.25), channel_id=1, source_target_pairs={{0,1},{1,2},{2,3},{3,4},{4,5},{5,6},{6,7},{7,8},{8,9},{9,10},{10,1... | collective-permute-start | bytes 1572872 | tf_op jit(solution)/shard_map/ppermute | solution.py:16
  314.8 27.1 %collective-permute-start.28 = (bf16[256,1024]{0,1:T(8,128)(2,1)}, bf16[256,1024]{0,1:T(8,128)(2,1)}, u32[]{:S(2)}, u32[]{:S(2)}) collective-permute-start(bf16[256,1024]{0,1:T(8,128)(2,1)} %collective-permute-done.26), channel_id=1, source_target_pairs={{0,1},{1,2},{2,3},{3,4},{4,5},{5,6},{6,7},{7,8},{8,9},{9,10},{10,1... | collective-permute-start | bytes 1572872 | tf_op jit(solution)/shard_map/ppermute | solution.py:16
  328.9 24.2 %collective-permute-start.29 = (bf16[256,1024]{1,0:T(8,128)(2,1)}, bf16[256,1024]{1,0:T(8,128)(2,1)}, u32[]{:S(2)}, u32[]{:S(2)}) collective-permute-start(bf16[256,1024]{1,0:T(8,128)(2,1)} %collective-permute-done.27), channel_id=1, source_target_pairs={{0,1},{1,2},{2,3},{3,4},{4,5},{5,6},{6,7},{7,8},{8,9},{9,10},{10,1... | collective-permute-start | bytes 1572872 | tf_op jit(solution)/shard_map/ppermute | solution.py:16
  341.9 22.1 %collective-permute-start.30 = (bf16[256,1024]{0,1:T(8,128)(2,1)}, bf16[256,1024]{0,1:T(8,128)(2,1)}, u32[]{:S(2)}, u32[]{:S(2)}) collective-permute-start(bf16[256,1024]{0,1:T(8,128)(2,1)} %collective-permute-done.28), channel_id=1, source_target_pairs={{0,1},{1,2},{2,3},{3,4},{4,5},{5,6},{6,7},{7,8},{8,9},{9,10},{10,1... | collective-permute-start | bytes 1572872 | tf_op jit(solution)/shard_map/ppermute | solution.py:16
  355.2 40.2 %collective-permute-start.31 = (bf16[256,1024]{1,0:T(8,128)(2,1)}, bf16[256,1024]{1,0:T(8,128)(2,1)}, u32[]{:S(2)}, u32[]{:S(2)}) collective-permute-start(bf16[256,1024]{1,0:T(8,128)(2,1)} %collective-permute-done.29), channel_id=1, source_target_pairs={{0,1},{1,2},{2,3},{3,4},{4,5},{5,6},{6,7},{7,8},{8,9},{9,10},{10,1... | collective-permute-start | bytes 1572872 | tf_op jit(solution)/shard_map/ppermute | solution.py:16
  (161 other events, 2124.9 us)
Sparse Core Ops, SparseCore 0:
  18.7 87.7 all-gather.2
where the time goes:
time: 586 us; the launch traced here: 575 us
  matrix products  252 us (43%)
  starting transfers between devices  115 us (20%)
  other arithmetic  81.2 us (14%)
  blocking collectives  66.8 us (11%)
  local copies, waits for them, and re-layouts  44 us (8%)
  between operations  16 us (3%)
    dot_general x17, matrix products, attend(): jnp.einsum('tgrd,sgd->tgrs', query_four, key_three, preferred_element_typ...  115 us
    ppermute x32, starting transfers between devices, from_behind(): return lax.ppermute(value, axis, pairs)  115 us
    dot_general x17, matrix products, attend(): jnp.einsum('tgrs,sgd->tgrd', weights.astype(jnp.bfloat16), value_three, p...  103 us
    all_gather x1, blocking collectives, per_device(): lax.all_gather(delta_norm[None].astype(jnp.bfloat16), 'seq', axis=0, tile...  66.8 us
    reduce_sum x9, other arithmetic, attend(): sum_total = sum_total * rescale + jnp.sum(weights, axis=-1)  59.4 us
    ppermute x16, local copies, waits for them, and re-layouts, from_behind(): return lax.ppermute(value, axis, pairs)  31.5 us
    dot_general x1, matrix products, per_device(): jnp.dot(mixed, out_weight, preferred_element_type=jnp.float32)  16.6 us
  transfers between devices with their start and end apart: 33, of which 0 were waited for; matrix products, arithmetic and copies ran while one was open for 55% of the time, Pallas kernels for 0%

commit v1 on v0

v1 whole, which is shorter than its diff:
```python
import functools
import math

import jax
import jax.numpy as jnp
from jax import lax
from jax.experimental import pallas as pl
from jax.experimental.pallas import tpu as pltpu
from jax.sharding import PartitionSpec as P

HDIM = 128
WINDOW = 4096
SEG = 1024
LOG2E = 1.4426950408889634
EXP_SCALE = LOG2E / math.sqrt(HDIM)


def feature(source):
    wide = source.astype(jnp.float32)
    low = jnp.exp(jnp.minimum(wide, 0.0))
    return jnp.where(wide > 0.0, wide + 1.0, low)


def kernel(
    size, group_size, gate_ref, q_ref, k_hbm, v_hbm, out_ref,
    kbuf, vbuf, m_ref, acc_ref, wsend, wrecv, dsum, dpre,
    local_sem, send_sem, recv_sem, zsend, zrecv, dsend, drecv,
):
    rows = q_ref.shape[0]
    width = kbuf.shape[2]
    groups = width // HDIM
    me = lax.axis_index("seq")
    plane = me // 8
    p = me % 8
    core = p % 2
    xbit = (p // 2) % 2
    ybit = p // 4
    base = me - p
    by_core = 1 - 2 * core
    by_x = 2 - 4 * xbit
    by_y = 4 - 8 * ybit
    dev_core, dev_x, dev_y = me + by_core, me + by_x, me + by_y
    slots = (p, p + by_x, p + by_y, p + by_x + by_y)
    bufs = (kbuf, vbuf)
    X_FIRST = ((True, True), (True, False), (True, False))

    has_up = me + 8 < size
    has_down = plane >= 1

    def rows_of(slot):
        return pl.ds(pl.multiple_of(slot * rows, rows), rows)

    def remote(src, dst, ssem, rsem, dev):
        return pltpu.make_async_remote_copy(
            src_ref=src, dst_ref=dst, send_sem=ssem, recv_sem=rsem,
            device_id={"seq": dev}, device_id_type=pl.DeviceIdType.MESH,
        )

    def hop(g, kv, slot, dev, idx):
        ref = bufs[kv].at[g, rows_of(slot), :]
        return remote(ref, ref, send_sem.at[g, kv, idx], recv_sem.at[g, kv, idx], dev)

    def up(g, kv):
        src = bufs[kv].at[g, rows_of(p), :]
        dst = bufs[kv].at[g + 1, rows_of(p), :]
        return remote(src, dst, zsend.at[g, kv], zrecv.at[g, kv], me + 8)

    def first_step(g, kv):
        return hop(g, kv, slots[0], dev_x if X_FIRST[g][kv] else dev_y, 0)

    def second_step(g, kv, which):
        if X_FIRST[g][kv]:
            return hop(g, kv, slots[(0, 1)[which]], dev_y, 1 + which)
        return hop(g, kv, slots[(0, 2)[which]], dev_x, 1 + which)

    def core_step(g, kv, which):
        return hop(g, kv, slots[which], dev_core, 3 + which)

    def sends_y(g):
        return (ybit == 0, ybit < 2, ybit == 1)[g]

    def far(g):
        return (ybit == 1, ybit < 2, ybit == 0)[g]

    def has(g):
        return plane >= g

    def conds(g, kv, idx):
        y_send, y_recv = has(g) & sends_y(g), has(g) & far(g)
        both = (has(g), has(g))
        if idx == 0:
            return both if X_FIRST[g][kv] else (y_send, y_recv)
        if idx in (1, 2):
            if X_FIRST[g][kv]:
                return (y_send, y_recv)
            return both if idx == 1 else (y_recv, y_recv)
        return both if idx in (3, 4) else (y_recv, y_recv)

    def copy_of(g, kv, idx):
        if idx == 0:
            return first_step(g, kv)
        if idx in (1, 2):
            return second_step(g, kv, idx - 1)
        return core_step(g, kv, idx - 3)

    def start(g, kv, idx):
        @pl.when(conds(g, kv, idx)[0])
        def _():
            copy_of(g, kv, idx).start()

    def arrive(g, kv, idx):
        @pl.when(conds(g, kv, idx)[1])
        def _():
            copy_of(g, kv, idx).wait_recv()

    def exchange(i, value):
        dev = (dev_core, dev_x, dev_y)[i]
        wsend[i] = value.astype(jnp.bfloat16)
        remote(wsend.at[i], wrecv.at[i], dsend.at[i], drecv.at[i], dev).start()

    def exchanged(i):
        dev = (dev_core, dev_x, dev_y)[i]
        remote(wsend.at[i], wrecv.at[i], dsend.at[i], drecv.at[i], dev).wait_recv()
        return wrecv[i].astype(jnp.float32)

    def chain():
        return remote(wsend.at[3], wrecv.at[3], dsend.at[3], drecv.at[3], me + 8)

    def attend(g, chunk, masked=False):
        first_row = pl.multiple_of(chunk * (2 * rows), 2 * rows)
        ones = jnp.ones((2 * rows, HDIM), jnp.bfloat16)
        if masked:
            qpos = lax.broadcasted_iota(jnp.int32, (rows, 2 * rows), 0) + p * rows
            kpos = lax.broadcasted_iota(jnp.int32, (rows, 2 * rows), 1) + first_row
            allowed = (qpos >= kpos) if g == 0 else (kpos > qpos)

        def head(h, carry):
            cols = pl.ds(pl.multiple_of(h * HDIM, HDIM), HDIM)
            k = kbuf[g, pl.ds(first_row, 2 * rows), cols]
            v = vbuf[g, pl.ds(first_row, 2 * rows), cols]
            v_wide = jnp.concatenate([v, ones], axis=1)
            for r in range(group_size):
                n = h * group_size + r
                q = q_ref[:, pl.ds(pl.multiple_of(n * HDIM, HDIM), HDIM)]
                s = lax.dot_general(
                    q, k, (((1,), (1,)), ((), ())), preferred_element_type=jnp.float32
                )
                if masked:
                    s = jnp.where(allowed, s, jnp.float32(-1e30))
                old = m_ref[n]
                new = jnp.maximum(old, jnp.max(s, axis=1, keepdims=True))
                m_ref[n] = new
                alpha = jnp.exp2((old - new) * EXP_SCALE)
                shift = jnp.concatenate([new] * (2 * rows // HDIM), axis=1)
                w = jnp.exp2((s - shift) * EXP_SCALE).astype(jnp.bfloat16)
                pv = jnp.dot(w, v_wide, preferred_element_type=jnp.float32)
                acc_ref[n] = acc_ref[n] * jnp.concatenate([alpha, alpha], axis=1) + pv
            return carry

        lax.fori_loop(0, groups, head, 0)

    own_chunk = p // 2
    near_chunk = own_chunk + 1 - 2 * xbit
    far_base = 2 - 2 * ybit
    KV = (0, 1)

    local = [
        pltpu.make_async_copy(hbm, buf.at[0, rows_of(p), :], local_sem.at[i])
        for i, (hbm, buf) in enumerate(((k_hbm, kbuf), (v_hbm, vbuf)))
    ]
    for c in local:
        c.start()
    barrier = pltpu.get_barrier_semaphore()
    for dev in (dev_core, dev_x, dev_y):
        pl.semaphore_signal(
            barrier, inc=1, device_id={"seq": dev}, device_id_type=pl.DeviceIdType.MESH
        )

    @pl.when(has_up)
    def _():
        pl.semaphore_signal(
            barrier, inc=1, device_id={"seq": me + 8}, device_id_type=pl.DeviceIdType.MESH
        )

    @pl.when(has_down)
    def _():
        pl.semaphore_signal(
            barrier, inc=1, device_id={"seq": me - 8}, device_id_type=pl.DeviceIdType.MESH
        )

    steps = max(size // 8 - 1, 1)
    neighbours_up = 1 - plane // steps if size > 8 else 0
    neighbours_down = (plane + steps - 1) // steps if size > 8 else 0
    pl.semaphore_wait(barrier, 3 + neighbours_up + jnp.minimum(neighbours_down, 1))

    for c in local:
        c.wait()

    for kv in KV:
        start(0, kv, 3)
    for kv in KV:
        @pl.when(has_up)
        def _(kv=kv):
            up(0, kv).start()

        start(0, kv, 0)
    m_ref[...] = jnp.full(m_ref.shape, -1e30, jnp.float32)
    acc_ref[...] = jnp.zeros(acc_ref.shape, jnp.float32)
    for h in range(groups):
        cols = slice(h * HDIM, (h + 1) * HDIM)
        kf = feature(kbuf[0, rows_of(p), cols]).astype(jnp.bfloat16)
        v = vbuf[0, rows_of(p), cols]
        dsum[0:HDIM, cols] = lax.dot_general(
            kf, v, (((0,), (0,)), ((), ())), preferred_element_type=jnp.float32
        )
        norm = jnp.sum(kf.astype(jnp.float32), axis=0, keepdims=True)
        dsum[HDIM:, cols] = jnp.broadcast_to(norm, (dsum.shape[0] - HDIM, HDIM))
    exchange(0, dsum[...])
    for kv in KV:
        arrive(0, kv, 3)
    attend(0, own_chunk, masked=True)
    dsum[...] += exchanged(0)
    exchange(1, dsum[...])

    for kv in KV:
        arrive(0, kv, 0)
        start(0, kv, 4)

    @pl.when(has(1))
    def _():
        for kv in KV:
            up(0, kv).wait_recv()

    for kv in KV:
        start(1, kv, 3)
        start(1, kv, 0)

        @pl.when(has(1) & has_up)
        def _(kv=kv):
            up(1, kv).start()

    for kv in KV:
        arrive(0, kv, 4)

    @pl.when(xbit == 1)
    def _():
        attend(0, near_chunk)

    for kv in KV:
        arrive(1, kv, 3)

    @pl.when(has(1))
    def _():
        attend(1, own_chunk)

    dsum[...] += exchanged(1)
    exchange(2, dsum[...])

    for kv in KV:
        arrive(1, kv, 0)
        start(1, kv, 1)
        start(1, kv, 2)
        start(1, kv, 4 if X_FIRST[1][kv] else 5)
    for kv in KV:
        start(0, kv, 1)
        start(0, kv, 2)

    @pl.when(has(2))
    def _():
        for kv in KV:
            up(1, kv).wait_recv()

    for kv in KV:
        start(2, kv, 3)
        start(2, kv, 0)
    other = exchanged(2)
    dpre[...] = other * ybit.astype(jnp.float32)
    dsum[...] += other

    @pl.when(has_up & (plane == 0))
    def _():
        wsend[3] = dsum[...].astype(jnp.bfloat16)
        chain().start()

    for kv in KV:
        arrive(2, kv, 3)

    @pl.when(has(2))
    def _():
        attend(2, own_chunk, masked=True)

    @pl.when(has_down)
    def _():
        chain().wait_recv()
        before = wrecv[3].astype(jnp.float32)
        dpre[...] += before

        @pl.when(has_up)
        def _():
            wsend[3] = (before + dsum[...]).astype(jnp.bfloat16)
            chain().start()

    for kv in KV:
        arrive(1, kv, 1)
        arrive(1, kv, 2)
        start(1, kv, 5 if X_FIRST[1][kv] else 4)
        start(1, kv, 6)
    for kv in KV:
        arrive(2, kv, 0)
        start(2, kv, 1)
        start(2, kv, 2)
        start(2, kv, 4 if X_FIRST[2][kv] else 5)
    for kv in KV:
        arrive(1, kv, 4)
        arrive(1, kv, 5)
        arrive(1, kv, 6)

    @pl.when(has(1))
    def _():
        def one(i, c):
            attend(1, (own_chunk + 1 + i) % 4)
            return c

        lax.fori_loop(0, 3, one, 0)

    for kv in KV:
        arrive(2, kv, 1)
        arrive(2, kv, 2)
        start(2, kv, 5 if X_FIRST[2][kv] else 4)
        start(2, kv, 6)
    for kv in KV:
        arrive(2, kv, 4)
        arrive(2, kv, 5)
        arrive(2, kv, 6)

    @pl.when(has(2) & (xbit == 0))
    def _():
        attend(2, near_chunk)

    for kv in KV:
        arrive(0, kv, 1)
        arrive(0, kv, 2)
        start(0, kv, 5)
        start(0, kv, 6)
    for kv in KV:
        arrive(0, kv, 5)
        arrive(0, kv, 6)

    @pl.when(far(0))
    def _():
        lax.fori_loop(0, 2, lambda i, c: (attend(0, far_base + i), c)[1], 0)

    @pl.when(has(2) & far(2))
    def _():
        lax.fori_loop(0, 2, lambda i, c: (attend(2, far_base + i), c)[1], 0)

    def finish(h, carry):
        cols = pl.ds(pl.multiple_of(h * HDIM, HDIM), HDIM)
        mem = dpre[0:HDIM, cols]
        high = mem.astype(jnp.bfloat16)
        low = (mem - high.astype(jnp.float32)).astype(jnp.bfloat16)
        norm = dpre[HDIM:HDIM + 1, cols]
        for r in range(group_size):
            n = h * group_size + r
            qcols = pl.ds(pl.multiple_of(n * HDIM, HDIM), HDIM)
            qf = feature(q_ref[:, qcols]).astype(jnp.bfloat16)
            recalled = jnp.dot(qf, high, preferred_element_type=jnp.float32) + jnp.dot(
                qf, low, preferred_element_type=jnp.float32
            )
            denominator = 1.0 + jnp.sum(qf.astype(jnp.float32) * norm, axis=1, keepdims=True)
            local_out = acc_ref[n, :, 0:HDIM] / acc_ref[n, :, HDIM:]
            share = gate_ref[n]
            mixed = share * (recalled / denominator) + (1.0 - share) * local_out
            out_ref[:, qcols] = mixed.astype(jnp.bfloat16)
        return carry

    lax.fori_loop(0, groups, finish, 0)

    for i, dev in enumerate((dev_core, dev_x, dev_y)):
        remote(wsend.at[i], wrecv.at[i], dsend.at[i], drecv.at[i], dev).wait_send()

    @pl.when(has_up)
    def _():
        chain().wait_send()
        for kv in KV:
            up(0, kv).wait_send()

    @pl.when(has_up & has(1))
    def _():
        for kv in KV:
            up(1, kv).wait_send()

    for g in range(3):
        for kv in KV:
            for idx in range(7):
                @pl.when(conds(g, kv, idx)[0])
                def _(g=g, kv=kv, idx=idx):
                    copy_of(g, kv, idx).wait_send()


def per_device(size, queries, keys, values, gate_logit, out_weight):
    rows = queries.shape[0]
    heads = gate_logit.shape[0]
    width = keys.shape[1]
    group_size = heads // (width // HDIM)
    assert WINDOW == 16 * rows and SEG == 4 * rows and size % 8 == 0
    vmem, anywhere = pl.BlockSpec(memory_space=pltpu.VMEM), pl.BlockSpec(memory_space=pl.ANY)
    mixed = pl.pallas_call(
        functools.partial(kernel, size, group_size),
        out_shape=jax.ShapeDtypeStruct(queries.shape, jnp.bfloat16),
        in_specs=[pl.BlockSpec(memory_space=pltpu.SMEM), vmem, anywhere, anywhere],
        out_specs=vmem,
        scratch_shapes=[
            pltpu.VMEM((3, 8 * rows, width), jnp.bfloat16),
            pltpu.VMEM((3, 8 * rows, width), jnp.bfloat16),
            pltpu.VMEM((heads, rows, HDIM), jnp.float32),
            pltpu.VMEM((heads, rows, 2 * HDIM), jnp.float32),
            pltpu.VMEM((4, HDIM + 16, width), jnp.bfloat16),
            pltpu.VMEM((4, HDIM + 16, width), jnp.bfloat16),
            pltpu.VMEM((HDIM + 16, width), jnp.float32),
            pltpu.VMEM((HDIM + 16, width), jnp.float32),
            pltpu.SemaphoreType.DMA((2,)),
            pltpu.SemaphoreType.DMA((3, 2, 7)),
            pltpu.SemaphoreType.DMA((3, 2, 7)),
            pltpu.SemaphoreType.DMA((2, 2)),
            pltpu.SemaphoreType.DMA((2, 2)),
            pltpu.SemaphoreType.DMA((4,)),
            pltpu.SemaphoreType.DMA((4,)),
        ],
        compiler_params=pltpu.CompilerParams(
            collective_id=0, has_side_effects=True, vmem_limit_bytes=60 * 1024 * 1024
        ),
    )(jax.nn.sigmoid(gate_logit), queries, keys, values)
    partial_value = jnp.dot(mixed, out_weight, preferred_element_type=jnp.float32)
    return lax.psum_scatter(
        partial_value.astype(jnp.bfloat16), "head", scatter_dimension=1, tiled=True
    )


def solution(mesh):
    in_specs = (P("seq", "head"), P("seq", "head"), P("seq", "head"), P("head"), P("head", None))
    out_specs = P("seq", "head")
    return jax.shard_map(
        functools.partial(per_device, mesh.shape["seq"]),
        mesh=mesh, in_specs=in_specs, out_specs=out_specs, check_vma=False,
    )
```

time: 586 us -> 162 us (0.28)
  the two profiles are of different devices: /device:TPU:0 before, /device:TPU:14 now
where the time goes in v1:
time: 162 us
  Pallas kernels  144 us (89%)
  matrix products  16.6 us (10%)
    pallas_call x1, Pallas kernels, per_device(): pl.pallas_call(functools.partial(kernel, size, group_size), out_shape=jax...  144 us
    dot_general x1, matrix products, per_device(): jnp.dot(mixed, out_weight, preferred_element_type=jnp.float32)  16.6 us

profile of v1, /device:TPU:14, one launch (start us, length us, event | category | flops | bytes accessed | tf_op | source)
XLA Modules:
  0.0 161.6 jit_solution(14804708225440435335)
XLA Ops:
  0.0 1.2 add_divide_fusion.gate_ref
  1.2 143.7 %shard_map.55 = bf16[256,4096]{1,0:T(8,128)(2,1)} custom-call(f32[32]{0:T(128)} %add_divide_fusion.gate_ref, bf16[256,4096]{1,0:T(8,128)(2,1)} %q_ref.1, bf16[256,1024]{1,0:T(8,128)(2,1)} %k_hbm.1, bf16[256,1024]{1,0:T(8,128)(2,1)} %v_hbm.1), custom_call_target="tpu_custom_call" | custom-call | tf_op jit(solution)/shard_map/pallas_call | solution.py:408
  144.9 16.6 %convolution_convert_fusion = bf16[256,4096]{1,0:T(8,128)(2,1)} fusion(bf16[256,4096]{1,0:T(8,128)(2,1)} %shard_map.55, bf16[4096,4096]{1,0:T(8,128)(2,1)} %param.9), kind=kOutput, calls=%fused_computation | convolution fusion | flops 8590983168 | bytes 37748736 | tf_op jit(solution)/shard_map/dot_general | solution.py:434
